TPU v7x, 32 devices: a whole 2x2x4 slice. The times are simulated.
32 devices in a mesh: ma: 8 (over z, x), band: 4 (over y, core).
Axes of the slice: x: 2, y: 2, z: 4, core: 2. Of those that a mesh axis runs over, the one named last changes fastest.
Arguments:
- observed: bfloat16 [256, 64, 1024], P(('ma', 'band')), may hold values from -6 to 6
- eigenvalues: float32 [256, 1024], P(('ma', 'band')), may hold values from 0.05 to 20
- kl_basis: bfloat16 [256, 1024, 512], P(('ma', 'band')), may hold values from -0.1875 to 0.1875
- band_deriv: bfloat16 [40, 512, 512], P('band'), may hold values from -0.15625 to 0.15625, as said below
- counts: int32 [256], P(('ma', 'band')), may hold values from 128 to 1024, as said below
Outputs:
- mode_power: float32 [256, 40], P('ma', 'band')
- band_power: float32 [40], P('band')
Inputs may be any that keep to these rules, and one draw needn't show every extreme that they name: counts[m] is the number of leading KL modes of m-mode m that are kept; some m-mode keeps 1024 and some keeps 1024 // 8. Each band_deriv[a] is symmetric.
All inputs are finite; a program needn't handle non-finite values.
Results may differ from a plain program's by a relative error of at most 0.0018.
Values may be sent and summed in bfloat16 or wider, within the bound.
No kernel may reach another device: no remote copies, remote signals or barrier semaphores. Data moves between devices by JAX's collectives and lax.ppermute only.
A program may use at most 64 MiB of HBM per device.

v0:
```python
import jax
import jax.numpy as jnp
from jax import lax
from jax.sharding import PartitionSpec as P


def weigh(observed, eigenvalues, counts):
    position = lax.broadcasted_iota(jnp.int32, eigenvalues.shape, 1)
    inside = position < counts[:, None]
    weights = jnp.where(inside, 1.0 / (1.0 + eigenvalues), jnp.zeros_like(eigenvalues))
    return (observed.astype(jnp.float32) * weights[:, None, :]).astype(jnp.bfloat16)


def project_padded(weighted, kl_basis):
    return jnp.einsum("msi,miw->msw", weighted, kl_basis, preferred_element_type=jnp.float32)


def band_quadratic(vectors, matrices):
    mode_count = vectors.shape[0]
    flattened = vectors.reshape(mode_count * vectors.shape[1], vectors.shape[2])

    def one_band(matrix):
        mapped = jnp.dot(flattened, matrix, preferred_element_type=jnp.float32)
        return jnp.sum((mapped * flattened).reshape(mode_count, -1), axis=1)

    return lax.map(one_band, matrices)


def per_device(observed, eigenvalues, kl_basis, band_deriv, counts):
    samples = observed.shape[1]
    live_total = lax.psum(jnp.sum(counts).astype(jnp.float32), ("ma", "band"))
    weighted = weigh(observed, eigenvalues, counts)
    projected = project_padded(weighted, kl_basis)
    projected = projected.astype(jnp.bfloat16)
    quadratic = band_quadratic(lax.all_gather(projected, "band", axis=0, tiled=True), band_deriv)
    mode_power = jnp.transpose(quadratic) / samples
    partial_sum = jnp.sum(mode_power, axis=0)
    band_total = lax.psum(partial_sum, "ma")
    band_power = observed.shape[2] * band_total / live_total
    return (mode_power, band_power)


def solution(mesh):
    in_specs = (
        P(("ma", "band"), None, None),
        P(("ma", "band"), None),
        P(("ma", "band"), None, None),
        P("band", None, None),
        P(("ma", "band")),
    )
    out_specs = (P("ma", "band"), P("band"))
    return jax.shard_map(
        per_device, mesh=mesh, in_specs=in_specs, out_specs=out_specs, check_vma=False
    )
```

profile of v0, /device:TPU:0, one launch (start us, length us, event | category | flops | bytes accessed | tf_op | source)
XLA Modules:
  0.0 117.1 jit_solution(10019816696674286477)
XLA Ops:
  7.2 0.0 all-gather.2.cloned.1.call-start
  7.2 0.8 divide_select_fusion
  8.0 0.0 copy-start
  8.0 6.0 %convolution_convert_fusion = bf16[8,64,512]{2,1,0:T(8,128)(2,1)} fusion(bf16[8,1024,512]{2,1,0:T(8,128)(2,1)} %param.9, bf16[8,64,1024]{2,1,0:T(8,128)(2,1)} %param.7, f32[8,1024]{1,0:T(8,128)S(1)} %divide_select_fusion), kind=kOutput, calls=%fused_computation.6 | convolution fusion | flops 538705920 | bytes 9994240 | tf_op jit(solution)/shard_map/msi,miw->msw/dot_general | solution.py:15
  14.1 0.0 all-gather.2.cloned.1.call-update
  14.1 0.0 copy-done
  14.1 0.6 reduce_sum.35
  15.4 42.4 %psum.15 = f32[]{:T(128)} all-reduce(f32[]{:T(128)S(6)} %convert_element_type.18), channel_id=1, replica_groups=mesh['ma'=8,'band'=4] {'ma','band'}, use_global_device_ids=true, to_apply=%region_7.8 | all-reduce | flops 1 | bytes 8 | tf_op jit(solution)/shard_map/psum | solution.py:31
  57.8 0.0 all-gather.2.cloned.1.call-done
  57.8 2.9 %copy.9 = bf16[2048,512]{0,1:T(8,128)(2,1)S(1)} copy(bf16[2048,512]{1,0:T(8,128)(2,1)} %bitcast.21) | data formatting | bytes 4194304 | tf_op jit(solution)/shard_map/while | solution.py:26
  60.8 26.6 %while.10 = (s32[]{:T(128)}, f32[10,32]{1,0:T(8,128)S(1)}, bf16[10,512,512]{2,1,0:T(8,128)(2,1)}, bf16[2048,512]{0,1:T(8,128)(2,1)S(1)}, s32[]{:T(128)}, /*index=5*/f32[]{:T(128)}, s32[]{:T(128)}) while((s32[]{:T(128)}, f32[10,32]{1,0:T(8,128)S(1)}, bf16[10,512,512]{2,1,0:T(8,128)(2,1)}, bf16[2048,512]{0,1:T(8,128)(2,1)S(1)}, s32[]{:T(128)}, ...), condition=%wide.region_3.4_spmd, body=%wide.region_0.3_spmd.sunk | while | flops 1076887552 | bytes 4752341 | solution.py:26
  60.8 2.4 %fusion.12 = f32[2048]{0:T(1024)S(1)} fusion(bf16[2048,512]{0,1:T(8,128)(2,1)S(1)} %get-tuple-element.89, bf16[10,512,512]{2,1,0:T(8,128)(2,1)} %get-tuple-element.88, s32[]{:T(128)} %get-tuple-element.79), kind=kOutput, calls=%fused_computation.1.clone.1 | convolution fusion | flops 1076885504 | bytes 4727296 | tf_op jit(solution)/shard_map/while/body/eval_jaxpr/dot_general | solution.py:23
  63.2 0.1 reduce_sum.42
  63.3 0.1 reduce_sum.43
  63.4 2.4 %fusion.12 = f32[2048]{0:T(1024)S(1)} fusion(bf16[2048,512]{0,1:T(8,128)(2,1)S(1)} %get-tuple-element.89, bf16[10,512,512]{2,1,0:T(8,128)(2,1)} %get-tuple-element.88, s32[]{:T(128)} %get-tuple-element.79), kind=kOutput, calls=%fused_computation.1.clone.1 | convolution fusion | flops 1076885504 | bytes 4727296 | tf_op jit(solution)/shard_map/while/body/eval_jaxpr/dot_general | solution.py:23
  65.9 0.1 reduce_sum.42
  65.9 0.1 reduce_sum.43
  66.1 2.4 %fusion.12 = f32[2048]{0:T(1024)S(1)} fusion(bf16[2048,512]{0,1:T(8,128)(2,1)S(1)} %get-tuple-element.89, bf16[10,512,512]{2,1,0:T(8,128)(2,1)} %get-tuple-element.88, s32[]{:T(128)} %get-tuple-element.79), kind=kOutput, calls=%fused_computation.1.clone.1 | convolution fusion | flops 1076885504 | bytes 4727296 | tf_op jit(solution)/shard_map/while/body/eval_jaxpr/dot_general | solution.py:23
  68.5 0.1 reduce_sum.42
  68.6 0.1 reduce_sum.43
  68.7 2.4 %fusion.12 = f32[2048]{0:T(1024)S(1)} fusion(bf16[2048,512]{0,1:T(8,128)(2,1)S(1)} %get-tuple-element.89, bf16[10,512,512]{2,1,0:T(8,128)(2,1)} %get-tuple-element.88, s32[]{:T(128)} %get-tuple-element.79), kind=kOutput, calls=%fused_computation.1.clone.1 | convolution fusion | flops 1076885504 | bytes 4727296 | tf_op jit(solution)/shard_map/while/body/eval_jaxpr/dot_general | solution.py:23
  71.2 0.1 reduce_sum.42
  71.2 0.1 reduce_sum.43
  71.4 2.4 %fusion.12 = f32[2048]{0:T(1024)S(1)} fusion(bf16[2048,512]{0,1:T(8,128)(2,1)S(1)} %get-tuple-element.89, bf16[10,512,512]{2,1,0:T(8,128)(2,1)} %get-tuple-element.88, s32[]{:T(128)} %get-tuple-element.79), kind=kOutput, calls=%fused_computation.1.clone.1 | convolution fusion | flops 1076885504 | bytes 4727296 | tf_op jit(solution)/shard_map/while/body/eval_jaxpr/dot_general | solution.py:23
  73.8 0.1 reduce_sum.42
  73.9 0.1 reduce_sum.43
  74.1 2.4 %fusion.12 = f32[2048]{0:T(1024)S(1)} fusion(bf16[2048,512]{0,1:T(8,128)(2,1)S(1)} %get-tuple-element.89, bf16[10,512,512]{2,1,0:T(8,128)(2,1)} %get-tuple-element.88, s32[]{:T(128)} %get-tuple-element.79), kind=kOutput, calls=%fused_computation.1.clone.1 | convolution fusion | flops 1076885504 | bytes 4727296 | tf_op jit(solution)/shard_map/while/body/eval_jaxpr/dot_general | solution.py:23
  76.5 0.1 reduce_sum.42
  76.5 0.1 reduce_sum.43
  76.7 2.4 %fusion.12 = f32[2048]{0:T(1024)S(1)} fusion(bf16[2048,512]{0,1:T(8,128)(2,1)S(1)} %get-tuple-element.89, bf16[10,512,512]{2,1,0:T(8,128)(2,1)} %get-tuple-element.88, s32[]{:T(128)} %get-tuple-element.79), kind=kOutput, calls=%fused_computation.1.clone.1 | convolution fusion | flops 1076885504 | bytes 4727296 | tf_op jit(solution)/shard_map/while/body/eval_jaxpr/dot_general | solution.py:23
  79.1 0.1 reduce_sum.42
  79.2 0.1 reduce_sum.43
  79.4 2.4 %fusion.12 = f32[2048]{0:T(1024)S(1)} fusion(bf16[2048,512]{0,1:T(8,128)(2,1)S(1)} %get-tuple-element.89, bf16[10,512,512]{2,1,0:T(8,128)(2,1)} %get-tuple-element.88, s32[]{:T(128)} %get-tuple-element.79), kind=kOutput, calls=%fused_computation.1.clone.1 | convolution fusion | flops 1076885504 | bytes 4727296 | tf_op jit(solution)/shard_map/while/body/eval_jaxpr/dot_general | solution.py:23
  81.8 0.1 reduce_sum.42
  81.9 0.1 reduce_sum.43
  82.0 2.4 %fusion.12 = f32[2048]{0:T(1024)S(1)} fusion(bf16[2048,512]{0,1:T(8,128)(2,1)S(1)} %get-tuple-element.89, bf16[10,512,512]{2,1,0:T(8,128)(2,1)} %get-tuple-element.88, s32[]{:T(128)} %get-tuple-element.79), kind=kOutput, calls=%fused_computation.1.clone.1 | convolution fusion | flops 1076885504 | bytes 4727296 | tf_op jit(solution)/shard_map/while/body/eval_jaxpr/dot_general | solution.py:23
  84.4 0.1 reduce_sum.42
  84.5 0.1 reduce_sum.43
  84.7 2.4 %fusion.12 = f32[2048]{0:T(1024)S(1)} fusion(bf16[2048,512]{0,1:T(8,128)(2,1)S(1)} %get-tuple-element.89, bf16[10,512,512]{2,1,0:T(8,128)(2,1)} %get-tuple-element.88, s32[]{:T(128)} %get-tuple-element.79), kind=kOutput, calls=%fused_computation.1.clone.1 | convolution fusion | flops 1076885504 | bytes 4727296 | tf_op jit(solution)/shard_map/while/body/eval_jaxpr/dot_general | solution.py:23
  87.1 0.1 reduce_sum.42
  87.2 0.1 reduce_sum.43
  87.3 0.7 multiply_reduce_fusion
  88.0 21.1 %psum.14 = f32[10]{0:T(128)S(1)} all-reduce(f32[10]{0:T(128)S(1)} %get-tuple-element.45), channel_id=1, replica_groups=mesh['ma'=8,'band'=4] {'ma'}, use_global_device_ids=true, to_apply=%region_5.6 | all-reduce | flops 10 | bytes 80 | tf_op jit(solution)/shard_map/psum | solution.py:38
  109.1 1.1 multiply_divide_fusion
  (11 shorter events, 0.3 us)
Async XLA Ops:
  7.2 50.7 %all-gather.2.cloned.1.call-start = ((), (), s32[]{:S(2)}) async-start(), calls=%async_computation | async-start | bytes 2621440 | tf_op jit(solution)/shard_map/all_gather | solution.py:35
  8.0 6.1 %copy-start = (s32[8]{0:T(128)S(1)}, s32[8]{0:T(128)}, u32[]{:S(2)}) copy-start(s32[8]{0:T(128)} %param.11) | copy-start | bytes 100
Sparse Core Ops, SparseCore 0:
  14.2 25.4 all-gather.1
where the time goes:
time: 118 us; the launch traced here: 117 us
  blocking collectives  63.5 us (54%)
  matrix products  30.2 us (26%)
  between operations  14.7 us (12%)
  other arithmetic  4.47 us (4%)
  local copies, waits for them, and re-layouts  3.98 us (3%)
    psum x1, blocking collectives, per_device(): live_total = lax.psum(jnp.sum(counts).astype(jnp.float32), ('ma', 'band'))  42.4 us
    dot_general x10, matrix products, one_band(): mapped = jnp.dot(flattened, matrix, preferred_element_type=jnp.float32)  24.1 us
    psum x1, blocking collectives, per_device(): band_total = lax.psum(partial_sum, 'ma')  21.1 us
    dot_general x1, matrix products, project_padded(): jnp.einsum('msi,miw->msw', weighted, kl_basis, preferred_element_type=jnp...  6.04 us
    while x1, local copies, waits for them, and re-layouts, band_quadratic(): return lax.map(one_band, matrices)  2.93 us
  transfers between devices with their start and end apart: 1, of which 0 were waited for; matrix products, arithmetic and copies ran while one was open for 1% of the time, Pallas kernels for 0%

commit v1 on v0

v1 whole, which is shorter than its diff:
```python
import functools

import jax
import jax.numpy as jnp
from jax import lax
from jax.experimental import pallas as pl
from jax.experimental.pallas import tpu as pltpu
from jax.sharding import PartitionSpec as P

DEPTH = 256
EXTRA = 16
BASE = 128
DIGITS = 3
LANES = 128


def project_kernel(first, counts, eigenvalues, observed, basis, out, held, rows, weighted, row_sem, held_sem):
    modes, samples, depth = rows.shape
    steps = depth // DEPTH

    def row_copy(m):
        return pltpu.make_async_copy(observed.at[first + m], rows.at[m], row_sem.at[m])

    def held_copy(m, k):
        part = pl.ds(k * DEPTH, DEPTH)
        return pltpu.make_async_copy(basis.at[first + m, part, :], held.at[m, k], held_sem.at[m, k])

    for m in range(modes):
        row_copy(m).start()
        for k in range(steps):

            @pl.when(k * DEPTH < counts[first + m])
            def _():
                held_copy(m, k).start()

    for m in range(modes):
        count = counts[first + m]
        row_copy(m).wait()
        values = eigenvalues[first + m : first + m + 1, :]
        position = lax.broadcasted_iota(jnp.int32, values.shape, 1)
        weights = jnp.where(position < count, 1.0 / (1.0 + values), jnp.zeros_like(values))
        scaled = (rows[m].astype(jnp.float32) * weights).astype(jnp.bfloat16)
        for k in range(steps):
            weighted[k] = scaled[:, k * DEPTH : (k + 1) * DEPTH]

        def step(k, total):
            held_copy(m, k).wait()
            return total + jnp.dot(weighted[k], held[m, k], preferred_element_type=jnp.float32)

        total = jnp.zeros((samples, out.shape[1]), jnp.float32)
        total = lax.fori_loop(0, (count + DEPTH - 1) // DEPTH, step, total)
        out[m * samples : (m + 1) * samples, :] = total.astype(jnp.bfloat16)

    live = counts[0]
    for m in range(1, counts.shape[0]):
        live = live + counts[m]
    row = lax.broadcasted_iota(jnp.int32, (EXTRA, out.shape[1]), 0)
    digits = jnp.zeros(row.shape, jnp.float32)
    for d in range(DIGITS):
        digit = lax.rem(lax.div(live, BASE**d), BASE)
        digits = jnp.where(row == d, digit.astype(jnp.float32), digits)
    out[modes * samples :, :] = digits.astype(jnp.bfloat16)


def project(first, modes, observed, eigenvalues, kl_basis, counts):
    _, samples, depth = observed.shape
    width = kl_basis.shape[2]
    steps = depth // DEPTH
    return pl.pallas_call(
        functools.partial(project_kernel, first),
        out_shape=jax.ShapeDtypeStruct((modes * samples + EXTRA, width), jnp.bfloat16),
        in_specs=[
            pl.BlockSpec(memory_space=pltpu.SMEM),
            pl.BlockSpec(memory_space=pltpu.VMEM),
            pl.BlockSpec(memory_space=pl.ANY),
            pl.BlockSpec(memory_space=pl.ANY),
        ],
        out_specs=pl.BlockSpec(memory_space=pltpu.VMEM),
        scratch_shapes=[
            pltpu.VMEM((modes, steps, DEPTH, width), jnp.bfloat16),
            pltpu.VMEM((modes, samples, depth), jnp.bfloat16),
            pltpu.VMEM((steps, samples, DEPTH), jnp.bfloat16),
            pltpu.SemaphoreType.DMA((modes,)),
            pltpu.SemaphoreType.DMA((modes, steps)),
        ],
        compiler_params=pltpu.CompilerParams(vmem_limit_bytes=16 * 2**20),
        cost_estimate=pl.CostEstimate(
            flops=2 * modes * samples * depth * width,
            bytes_accessed=2 * modes * depth * (width + samples),
            transcendentals=0,
        ),
        name="project",
    )(counts, eigenvalues, observed, kl_basis)


def quadratic_kernel(sizes, samples, counted, matrices, *refs):
    blocks, out, doubled, wide = refs[: len(sizes)], refs[len(sizes)], refs[-2], refs[-1]
    bands, width, _ = matrices.shape
    half = width // 2
    starts = [sum(sizes[:b]) for b in range(len(sizes))]
    for block, modes, start in zip(blocks, sizes, starts):
        rows = slice(start * samples, (start + modes) * samples)
        left = block[: modes * samples, :half]
        right = block[: modes * samples, half:]
        doubled[rows, :half] = left + left
        doubled[rows, half:] = right
        wide[rows, :half] = left.astype(jnp.float32)
        wide[rows, half:] = right.astype(jnp.float32)

    lane = lax.broadcasted_iota(jnp.int32, (1, LANES), 1)

    def band(a, results):
        updated = []
        for block, modes, start, result in zip(blocks, sizes, starts, results):
            rows = slice(start * samples, (start + modes) * samples)
            first = jnp.dot(
                block[: modes * samples, :half], matrices[a, :half, :half], preferred_element_type=jnp.float32
            )
            second = jnp.dot(doubled[rows, :], matrices[a, :, half:], preferred_element_type=jnp.float32)
            terms = first * wide[rows, :half] + second * wide[rows, half:]
            folded = terms[:, :LANES]
            for k in range(1, half // LANES):
                folded = folded + terms[:, k * LANES : (k + 1) * LANES]
            power = jnp.sum(jnp.sum(folded.reshape(modes, samples, LANES), axis=1), axis=1, keepdims=True)
            updated.append(jnp.where(lane == a, power / samples, result))
        return tuple(updated)

    results = tuple(jnp.zeros((modes, LANES), jnp.float32) for modes in sizes)
    results = lax.fori_loop(0, bands, band, results)
    for b, (block, modes, start, result) in enumerate(zip(blocks, sizes, starts, results)):
        if b in counted:
            digits = block[modes * samples :, :LANES].astype(jnp.float32)
            live = digits[0:1, :]
            for d in range(1, DIGITS):
                live = live + float(BASE**d) * digits[d : d + 1, :]
            mode = lax.broadcasted_iota(jnp.int32, (modes, LANES), 0)
            result = jnp.where((mode == 0) & (lane == bands), live, result)
        out[start : start + modes, :] = result


def quadratic(blocks, samples, counted, matrices):
    bands, width, _ = matrices.shape
    sizes = tuple((block.shape[0] - EXTRA) // samples for block in blocks)
    modes = sum(sizes)
    return pl.pallas_call(
        functools.partial(quadratic_kernel, sizes, samples, counted),
        out_shape=jax.ShapeDtypeStruct((modes, LANES), jnp.float32),
        in_specs=[pl.BlockSpec(memory_space=pltpu.VMEM)] * (1 + len(blocks)),
        out_specs=pl.BlockSpec(memory_space=pltpu.VMEM),
        scratch_shapes=[
            pltpu.VMEM((modes * samples, width), jnp.bfloat16),
            pltpu.VMEM((modes * samples, width), jnp.float32),
        ],
        compiler_params=pltpu.CompilerParams(vmem_limit_bytes=24 * 2**20),
        cost_estimate=pl.CostEstimate(
            flops=2 * bands * modes * samples * width * width,
            bytes_accessed=2 * modes * samples * width,
            transcendentals=0,
        ),
        name="quadratic",
    )(matrices, *blocks)


def collect_kernel(groups, chunk_sizes, bands, *refs):
    results, power, sums, ordered = refs[: len(groups)], refs[-3], refs[-2], refs[-1]
    me = lax.axis_index("band")
    total = sum(chunk_sizes)
    for result, entries in zip(results, groups):
        at = 0
        for offset, chunk in entries:
            modes = chunk_sizes[chunk]
            place = lax.bitwise_xor(me, offset) * total + sum(chunk_sizes[:chunk])
            ordered[pl.ds(place, modes), :] = result[at : at + modes, :]
            at += modes
    values = ordered[...]
    power[...] = jnp.transpose(values)[:bands, :]
    sums[...] = jnp.sum(values, axis=0, keepdims=True)


def collect(results, groups, chunk_sizes, bands, blocks):
    modes = sum(chunk_sizes) * blocks
    return pl.pallas_call(
        functools.partial(collect_kernel, groups, chunk_sizes, bands),
        out_shape=(
            jax.ShapeDtypeStruct((bands, modes), jnp.float32),
            jax.ShapeDtypeStruct((1, LANES), jnp.float32),
        ),
        in_specs=[pl.BlockSpec(memory_space=pltpu.VMEM)] * len(results),
        out_specs=(pl.BlockSpec(memory_space=pltpu.VMEM),) * 2,
        scratch_shapes=[pltpu.VMEM((modes, LANES), jnp.float32)],
        name="collect",
    )(*results)


def normalize_kernel(bands, scale, mine, other, out):
    total = mine[...] + other[...]
    out[...] = scale * total[:, :bands] / total[:, bands : bands + 1]


def per_device(ma, band, observed, eigenvalues, kl_basis, band_deriv, counts):
    own_modes, samples, depth = observed.shape
    bands = band_deriv.shape[0]
    chunk_sizes = (own_modes // 2, own_modes - own_modes // 2)
    last = len(chunk_sizes) - 1

    def swap(array, axis, size, bit):
        return lax.ppermute(array, axis, [(i, i ^ bit) for i in range(size)])

    held = {}
    first = 0
    for c, modes in enumerate(chunk_sizes):
        held[0, c] = project(first, modes, observed, eigenvalues, kl_basis, counts)
        first += modes
    bits = []
    bit = band // 2
    while bit:
        bits.append(bit)
        bit //= 2

    known = [0]
    far = bits[0]
    for c in range(len(chunk_sizes)):
        held[far, c] = swap(held[0, c], "band", band, far)
    near = [0]
    for bit in bits[1:]:
        for offset in list(near):
            for c in range(len(chunk_sizes)):
                held[offset ^ bit, c] = swap(held[offset, c], "band", band, bit)
            near.append(offset ^ bit)
    for c in range(len(chunk_sizes)):
        arrived = [far]
        for bit in bits[1:]:
            for offset in list(arrived):
                held[offset ^ bit, c] = swap(held[offset, c], "band", band, bit)
                arrived.append(offset ^ bit)

    groups = [tuple((offset, c) for offset in near for c in range(len(chunk_sizes)))]
    for c in range(len(chunk_sizes)):
        for offset in near:
            groups.append(((offset ^ far, c),))
    results = []
    for entries in groups:
        counted = tuple(e for e, (_, c) in enumerate(entries) if c == last)
        results.append(quadratic([held[entry] for entry in entries], samples, counted, band_deriv))
    power, sums = collect(results, tuple(groups), chunk_sizes, bands, band)

    bit = 1
    while bit < ma:
        other = swap(sums, "ma", ma, bit)
        if 2 * bit < ma:
            sums = sums + other
        bit *= 2
    total = pl.pallas_call(
        functools.partial(normalize_kernel, bands, float(depth)),
        out_shape=jax.ShapeDtypeStruct((1, bands), jnp.float32),
        name="normalize",
    )(sums, other)
    return jnp.transpose(power), total.reshape(bands)


def solution(mesh):
    in_specs = (
        P(("ma", "band"), None, None),
        P(("ma", "band"), None),
        P(("ma", "band"), None, None),
        P("band", None, None),
        P(("ma", "band")),
    )
    out_specs = (P("ma", "band"), P("band"))
    body = functools.partial(per_device, mesh.shape["ma"], mesh.shape["band"])
    return jax.shard_map(body, mesh=mesh, in_specs=in_specs, out_specs=out_specs, check_vma=False)
```

time: 118 us -> 65.4 us (0.55)
  blocking collectives: 63.5 us -> 0 us
  Pallas kernels: 0 us -> 32.1 us
  matrix products: 30.2 us -> 0 us
  between operations: 14.7 us -> 0.74 us
  waiting for transfers between devices: 0.02 us -> 13.4 us
  starting transfers between devices: 0.04 us -> 10.3 us
  local copies, waits for them, and re-layouts: 3.98 us -> 7.81 us
  other arithmetic: 4.47 us -> 0.66 us
    psum x2 -> x0, blocking collectives: 63.5 us -> none  [the longest x1 42.4 us: per_device(): live_total = lax.psum(jnp.sum(counts).astype(jnp.float32), ('ma', 'band'))]
    pallas_call x0 -> x9, Pallas kernels: none -> 32.1 us  [the longest x5 21.8 us: quadratic(): pl.pallas_call(functools.partial(quadratic_kernel, sizes, samples, counte...]
    dot_general x11 -> x0, matrix products: 30.2 us -> none  [the longest x10 24.1 us: one_band(): mapped = jnp.dot(flattened, matrix, preferred_element_type=jnp.float32)]
    ppermute x0 -> x9, waiting for transfers between devices: none -> 13.4 us  [swap(): return lax.ppermute(array, axis, [(i, i ^ bit) for i in range(size)])]
    ppermute x0 -> x9, starting transfers between devices: none -> 10.3 us  [swap(): return lax.ppermute(array, axis, [(i, i ^ bit) for i in range(size)])]
    unnamed x2 -> x26, local copies, waits for them, and re-layouts: 0.01 us -> 7.81 us
    while x1 -> x0, local copies, waits for them, and re-layouts: 2.93 us -> none  [band_quadratic(): return lax.map(one_band, matrices)]
    reduce_sum x12 -> x0, other arithmetic: 2.5 us -> none  [the longest x10 1.16 us: one_band(): return jnp.sum((mapped * flattened).reshape(mode_count, -1), axis=1)]
  transfers between devices with their start and end apart: 1 -> 9, of which waited for: 0 -> 5; matrix products, arithmetic and copies ran while one was open for 1% -> 0% of each run, Pallas kernels for 0% -> 34%
where the time goes in v1:
time: 65.4 us; the launch traced here: 65 us
  Pallas kernels  32.1 us (49%)
  waiting for transfers between devices  13.4 us (20%)
  starting transfers between devices  10.3 us (16%)
  local copies, waits for them, and re-layouts  7.81 us (12%)
  between operations  0.74 us (1%)
  other arithmetic  0.66 us (1%)
    pallas_call x5, Pallas kernels, quadratic(): pl.pallas_call(functools.partial(quadratic_kernel, sizes, samples, counte...  21.8 us
    ppermute x9, waiting for transfers between devices, swap(): return lax.ppermute(array, axis, [(i, i ^ bit) for i in range(size)])  13.4 us
    ppermute x9, starting transfers between devices, swap(): return lax.ppermute(array, axis, [(i, i ^ bit) for i in range(size)])  10.3 us
    unnamed x26, local copies, waits for them, and re-layouts  7.81 us
    pallas_call x2, Pallas kernels, project(): pl.pallas_call(functools.partial(project_kernel, first), out_shape=jax.Sh...  7.65 us
    pallas_call x1, Pallas kernels, collect(): pl.pallas_call(functools.partial(collect_kernel, groups, chunk_sizes, ban...  1.39 us
  transfers between devices with their start and end apart: 9, of which 5 were waited for; matrix products, arithmetic and copies ran while one was open for 0% of the time, Pallas kernels for 34%

profile of v1, /device:TPU:0, one launch (start us, length us, event | category | flops | bytes accessed | tf_op | source)
XLA Modules:
  0.0 65.0 jit_solution(13014503384721856114)
XLA Ops:
  0.6 0.0 copy-start
  0.6 3.4 %copy-done = bf16[8,1024,512]{2,1,0:T(8,128)(2,1)S(1)} copy-done((bf16[8,1024,512]{2,1,0:T(8,128)(2,1)S(1)}, bf16[8,1024,512]{2,1,0:T(8,128)(2,1)}, u32[]{:S(2)}) %copy-start) | copy-done | bytes 8388632
  4.0 0.0 copy-start.1
  4.0 1.2 %copy-done.1 = bf16[8,64,1024]{2,1,0:T(8,128)(2,1)S(1)} copy-done((bf16[8,64,1024]{2,1,0:T(8,128)(2,1)S(1)}, bf16[8,64,1024]{2,1,0:T(8,128)(2,1)}, u32[]{:S(2)}) %copy-start.1) | copy-done | bytes 1048600
  5.2 0.0 copy-start.2
  5.2 0.8 %copy-done.2 = f32[8,1024]{1,0:T(8,128)S(1)} copy-done((f32[8,1024]{1,0:T(8,128)S(1)}, f32[8,1024]{1,0:T(8,128)}, u32[]{:S(2)}) %copy-start.2) | copy-done | bytes 32792
  6.0 0.0 copy-start.8
  6.0 0.7 %copy-done.8 = s32[8]{0:T(128)S(1)} copy-done((s32[8]{0:T(128)S(1)}, s32[8]{0:T(128)}, u32[]{:S(2)}) %copy-start.8) | copy-done | bytes 56
  6.7 0.0 slice-start
  6.7 3.7 %project.2.refs_0_ = bf16[272,512]{1,0:T(8,128)(2,1)S(1)} custom-call(s32[8]{0:T(128)S(1)} %copy-done.8, f32[8,1024]{1,0:T(8,128)S(1)} %copy-done.2, bf16[8,64,1024]{2,1,0:T(8,128)(2,1)S(1)} %copy-done.1, bf16[8,1024,512]{2,1,0:T(8,128)(2,1)S(1)} %copy-done), custom_call_target="tpu_custom_call" | custom-call | flops 268435456 | bytes 4718592 | tf_op jit(solution)/shard_map/project/pallas_call | solution.py:69
  10.4 0.0 slice-start.1
  10.4 2.9 %collective-permute-start.2 = (bf16[272,512]{1,0:T(8,128)(2,1)S(1)}, bf16[272,512]{1,0:T(8,128)(2,1)S(1)}, u32[]{:S(2)}, u32[]{:S(2)}) collective-permute-start(bf16[272,512]{1,0:T(8,128)(2,1)S(1)} %project.2.refs_0_), channel_id=1, source_target_pairs={{0,2},{1,3},{2,0},{3,1},{4,6},{5,7},{6,4},{7,5},{8,10},{9,11},{10,... | collective-permute-start | bytes 835592 | tf_op jit(solution)/shard_map/ppermute | solution.py:207
  13.3 3.9 %project.3.refs_1_ = bf16[272,512]{1,0:T(8,128)(2,1)S(1)} custom-call(s32[8]{0:T(128)S(1)} %copy-done.8, f32[8,1024]{1,0:T(8,128)S(1)} %copy-done.2, bf16[8,64,1024]{2,1,0:T(8,128)(2,1)S(1)} %copy-done.1, bf16[8,1024,512]{2,1,0:T(8,128)(2,1)S(1)} %copy-done), custom_call_target="tpu_custom_call" | custom-call | flops 268435456 | bytes 4718592 | tf_op jit(solution)/shard_map/project/pallas_call | solution.py:69
  17.2 0.1 collective-permute-start.4
  17.3 0.1 collective-permute-start
  17.4 0.5 collective-permute-start.1
  17.9 2.9 %collective-permute-done.2.refs_0_ = bf16[272,512]{1,0:T(8,128)(2,1)S(1)} collective-permute-done((bf16[272,512]{1,0:T(8,128)(2,1)S(1)}, bf16[272,512]{1,0:T(8,128)(2,1)S(1)}, u32[]{:S(2)}, u32[]{:S(2)}) %collective-permute-start.2) | collective-permute-done | bytes 278560 | tf_op jit(solution)/shard_map/ppermute | solution.py:207
  20.8 0.0 collective-permute-start.3
  20.8 4.9 %collective-permute-done.4.refs_0_ = bf16[272,512]{1,0:T(8,128)(2,1)S(1)} collective-permute-done((bf16[272,512]{1,0:T(8,128)(2,1)S(1)}, bf16[272,512]{1,0:T(8,128)(2,1)S(1)}, u32[]{:S(2)}, u32[]{:S(2)}) %collective-permute-start.4) | collective-permute-done | bytes 278560 | tf_op jit(solution)/shard_map/ppermute | solution.py:207
  25.7 0.0 collective-permute-start.5
  25.7 0.0 collective-permute-done.refs_2_
  25.7 0.0 collective-permute-done.1.refs_3_
  25.7 0.0 slice-done
  25.7 0.0 slice-done.1
  25.8 7.2 %quadratic.5.refs_0_ = f32[16,128]{1,0:T(8,128)S(1)} custom-call(bf16[10,512,512]{2,1,0:T(8,128)(2,1)S(1)} %bitcast.3, bf16[272,512]{1,0:T(8,128)(2,1)S(1)} %project.2.refs_0_, bf16[272,512]{1,0:T(8,128)(2,1)S(1)} %project.3.refs_1_, bf16[272,512]{1,0:T(8,128)(2,1)S(1)} %collective-permute-done.refs_2_, bf16[272,512]{1,0:T(8,128)(2,1)S(1)} %collective-permute-done.1.refs_3_), custom_call_target="tpu_custom_call" | custom-call | flops 5368709120 | bytes 1048576 | tf_op jit(solution)/shard_map/quadratic/pallas_call | solution.py:145
  32.9 0.0 copy-start.7
  32.9 3.7 %quadratic.6.refs_1_ = f32[4,128]{1,0:T(4,128)S(1)} custom-call(bf16[10,512,512]{2,1,0:T(8,128)(2,1)S(1)} %bitcast.3, bf16[272,512]{1,0:T(8,128)(2,1)S(1)} %collective-permute-done.2.refs_0_), custom_call_target="tpu_custom_call" | custom-call | flops 1342177280 | bytes 262144 | tf_op jit(solution)/shard_map/quadratic/pallas_call | solution.py:145
  36.6 0.0 copy-start.3
  36.6 3.7 %quadratic.8.refs_3_ = f32[4,128]{1,0:T(4,128)S(1)} custom-call(bf16[10,512,512]{2,1,0:T(8,128)(2,1)S(1)} %bitcast.3, bf16[272,512]{1,0:T(8,128)(2,1)S(1)} %collective-permute-done.4.refs_0_), custom_call_target="tpu_custom_call" | custom-call | flops 1342177280 | bytes 262144 | tf_op jit(solution)/shard_map/quadratic/pallas_call | solution.py:145
  40.2 0.0 copy-start.4
  40.2 0.0 collective-permute-done.3.refs_0_
  40.2 3.6 %quadratic.7.refs_2_ = f32[4,128]{1,0:T(4,128)S(1)} custom-call(bf16[10,512,512]{2,1,0:T(8,128)(2,1)S(1)} %bitcast.3, bf16[272,512]{1,0:T(8,128)(2,1)S(1)} %collective-permute-done.3.refs_0_), custom_call_target="tpu_custom_call" | custom-call | flops 1342177280 | bytes 262144 | tf_op jit(solution)/shard_map/quadratic/pallas_call | solution.py:145
  43.9 0.0 copy-start.5
  43.9 0.6 copy-done.5
  44.5 0.0 collective-permute-done.5.refs_0_
  44.5 0.0 copy-done.7
  44.5 0.0 copy-done.3
  44.5 0.0 copy-done.4
  44.5 3.6 %quadratic.9.refs_4_ = f32[4,128]{1,0:T(4,128)S(1)} custom-call(bf16[10,512,512]{2,1,0:T(8,128)(2,1)S(1)} %bitcast.3, bf16[272,512]{1,0:T(8,128)(2,1)S(1)} %collective-permute-done.5.refs_0_), custom_call_target="tpu_custom_call" | custom-call | flops 1342177280 | bytes 262144 | tf_op jit(solution)/shard_map/quadratic/pallas_call | solution.py:145
  48.2 0.0 copy-start.6
  48.2 0.6 copy-done.6
  48.7 1.4 %collect.1 = (f32[10,32]{1,0:T(8,128)}, f32[1,128]{1,0:T(1,128)}) custom-call(f32[16,128]{1,0:T(8,128)} %copy-done.7, f32[4,128]{1,0:T(4,128)} %copy-done.3, f32[4,128]{1,0:T(4,128)} %copy-done.5, f32[4,128]{1,0:T(4,128)} %copy-done.4, f32[4,128]{1,0:T(4,128)} %copy-done.6), custom_call_target="tpu_custom_call" | custom-call | tf_op jit(solution)/shard_map/collect/pallas_call | solution.py:182
  50.1 2.6 %collective-permute-start.6 = (f32[1,128]{1,0:T(1,128)}, f32[1,128]{1,0:T(1,128)S(1)}, u32[]{:S(2)}, u32[]{:S(2)}) collective-permute-start(f32[1,128]{1,0:T(1,128)} %get-tuple-element.5), channel_id=1, source_target_pairs={{0,4},{4,0},{8,12},{12,8},{16,20},{20,16},{24,28},{28,24},{1,5},{5... | collective-permute-start | bytes 1544 | tf_op jit(solution)/shard_map/ppermute | solution.py:207
  52.7 1.7 %collective-permute-done.6 = f32[1,128]{1,0:T(1,128)S(1)} collective-permute-done((f32[1,128]{1,0:T(1,128)}, f32[1,128]{1,0:T(1,128)S(1)}, u32[]{:S(2)}, u32[]{:S(2)}) %collective-permute-start.6) | collective-permute-done | bytes 544 | tf_op jit(solution)/shard_map/ppermute | solution.py:207
  54.4 0.7 %add.6 = f32[1,128]{1,0:T(1,128)S(1)} add(f32[1,128]{1,0:T(1,128)} %get-tuple-element.5, f32[1,128]{1,0:T(1,128)S(1)} %collective-permute-done.6) | non-fusion elementwise | flops 128 | bytes 1536 | tf_op jit(solution)/shard_map/add | solution.py:251
  55.1 1.8 %collective-permute-start.7 = (f32[1,128]{1,0:T(1,128)S(1)}, f32[1,128]{1,0:T(1,128)S(1)}, u32[]{:S(2)}, u32[]{:S(2)}) collective-permute-start(f32[1,128]{1,0:T(1,128)S(1)} %add.6), channel_id=1, source_target_pairs={{0,8},{4,12},{8,0},{12,4},{16,24},{20,28},{24,16},{28,20},{1,9},{5... | collective-permute-start | bytes 1544 | tf_op jit(solution)/shard_map/ppermute | solution.py:207
  56.8 1.8 %collective-permute-done.7 = f32[1,128]{1,0:T(1,128)S(1)} collective-permute-done((f32[1,128]{1,0:T(1,128)S(1)}, f32[1,128]{1,0:T(1,128)S(1)}, u32[]{:S(2)}, u32[]{:S(2)}) %collective-permute-start.7) | collective-permute-done | bytes 544 | tf_op jit(solution)/shard_map/ppermute | solution.py:207
  58.6 0.0 copy-start.9
  58.6 2.4 %collective-permute-start.8 = (f32[1,128]{1,0:T(1,128)S(1)}, f32[1,128]{1,0:T(1,128)S(1)}, u32[]{:S(2)}, u32[]{:S(2)}) collective-permute-start(f32[1,128]{1,0:T(1,128)S(1)} %add.7.mine), channel_id=1, source_target_pairs={{0,16},{4,20},{8,24},{12,28},{16,0},{20,4},{24,8},{28,12},{1,17},{... | collective-permute-start | bytes 1544 | tf_op jit(solution)/shard_map/ppermute | solution.py:207
  61.0 2.1 %collective-permute-done.8.other = f32[1,128]{1,0:T(1,128)S(1)} collective-permute-done((f32[1,128]{1,0:T(1,128)S(1)}, f32[1,128]{1,0:T(1,128)S(1)}, u32[]{:S(2)}, u32[]{:S(2)}) %collective-permute-start.8) | collective-permute-done | bytes 544 | tf_op jit(solution)/shard_map/ppermute | solution.py:207
  63.1 0.0 copy-done.9
  63.1 0.0 copy-start.10
  63.1 0.6 copy-done.10
  63.7 1.3 %normalize.1 = f32[1,10]{1,0:T(1,128)} custom-call(f32[1,128]{1,0:T(1,128)} %copy-done.9, f32[1,128]{1,0:T(1,128)} %copy-done.10), custom_call_target="tpu_custom_call" | custom-call | tf_op jit(solution)/shard_map/normalize/pallas_call | solution.py:253
  (2 shorter events, 0.0 us)
Async XLA Ops:
  0.6 3.4 %copy-start = (bf16[8,1024,512]{2,1,0:T(8,128)(2,1)S(1)}, bf16[8,1024,512]{2,1,0:T(8,128)(2,1)}, u32[]{:S(2)}) copy-start(bf16[8,1024,512]{2,1,0:T(8,128)(2,1)} %basis.3) | copy-start | bytes 25165828
  4.0 1.2 %copy-start.1 = (bf16[8,64,1024]{2,1,0:T(8,128)(2,1)S(1)}, bf16[8,64,1024]{2,1,0:T(8,128)(2,1)}, u32[]{:S(2)}) copy-start(bf16[8,64,1024]{2,1,0:T(8,128)(2,1)} %observed.3) | copy-start | bytes 3145732
  5.2 0.8 %copy-start.2 = (f32[8,1024]{1,0:T(8,128)S(1)}, f32[8,1024]{1,0:T(8,128)}, u32[]{:S(2)}) copy-start(f32[8,1024]{1,0:T(8,128)} %eigenvalues.3) | copy-start | bytes 98308
  6.0 0.7 %copy-start.8 = (s32[8]{0:T(128)S(1)}, s32[8]{0:T(128)}, u32[]{:S(2)}) copy-start(s32[8]{0:T(128)} %counts.3) | copy-start | bytes 100
  6.7 19.1 %slice-start = ((s8[5242880]{0:T(1024)(128)(4,1)}), s8[4194304]{0:T(1024)(128)(4,1)S(1)}, s32[]{:S(2)}) async-start(s8[5242880]{0:T(1024)(128)(4,1)} %bitcast.2), calls=%async_computation | async-start | bytes 8388608
  10.4 15.4 %slice-start.1 = ((s8[5242880]{0:T(1024)(128)(4,1)}), s8[1048576]{0:T(1024)(128)(4,1)S(1)}, s32[]{:S(2)}) async-start(s8[5242880]{0:T(1024)(128)(4,1)} %bitcast.2), calls=%async_computation.1 | async-start | bytes 2097152
  10.4 10.4 %collective-permute-start.2 = (bf16[272,512]{1,0:T(8,128)(2,1)S(1)}, bf16[272,512]{1,0:T(8,128)(2,1)S(1)}, u32[]{:S(2)}, u32[]{:S(2)}) collective-permute-start(bf16[272,512]{1,0:T(8,128)(2,1)S(1)} %project.2.refs_0_), channel_id=1, source_target_pairs={{0,2},{1,3},{2,0},{3,1},{4,6},{5,7},{6,4},{7,5},{8,10},{9,11},{10,... | collective-permute-start | bytes 835592 | tf_op jit(solution)/shard_map/ppermute | solution.py:207
  17.2 8.5 %collective-permute-start.4 = (bf16[272,512]{1,0:T(8,128)(2,1)S(1)}, bf16[272,512]{1,0:T(8,128)(2,1)S(1)}, u32[]{:S(2)}, u32[]{:S(2)}) collective-permute-start(bf16[272,512]{1,0:T(8,128)(2,1)S(1)} %project.3.refs_1_), channel_id=1, source_target_pairs={{0,2},{1,3},{2,0},{3,1},{4,6},{5,7},{6,4},{7,5},{8,10},{9,11},{10,... | collective-permute-start | bytes 835592 | tf_op jit(solution)/shard_map/ppermute | solution.py:207
  17.3 8.4 %collective-permute-start = (bf16[272,512]{1,0:T(8,128)(2,1)S(1)}, bf16[272,512]{1,0:T(8,128)(2,1)S(1)}, u32[]{:S(2)}, u32[]{:S(2)}) collective-permute-start(bf16[272,512]{1,0:T(8,128)(2,1)S(1)} %project.2.refs_0_), channel_id=1, source_target_pairs={{0,1},{1,0},{2,3},{3,2},{4,5},{5,4},{6,7},{7,6},{8,9},{9,8},{10,11... | collective-permute-start | bytes 835592 | tf_op jit(solution)/shard_map/ppermute | solution.py:207
  17.4 8.4 %collective-permute-start.1 = (bf16[272,512]{1,0:T(8,128)(2,1)S(1)}, bf16[272,512]{1,0:T(8,128)(2,1)S(1)}, u32[]{:S(2)}, u32[]{:S(2)}) collective-permute-start(bf16[272,512]{1,0:T(8,128)(2,1)S(1)} %project.3.refs_1_), channel_id=1, source_target_pairs={{0,1},{1,0},{2,3},{3,2},{4,5},{5,4},{6,7},{7,6},{8,9},{9,8},{10,11... | collective-permute-start | bytes 835592 | tf_op jit(solution)/shard_map/ppermute | solution.py:207
  20.8 19.4 %collective-permute-start.3 = (bf16[272,512]{1,0:T(8,128)(2,1)S(1)}, bf16[272,512]{1,0:T(8,128)(2,1)S(1)}, u32[]{:S(2)}, u32[]{:S(2)}) collective-permute-start(bf16[272,512]{1,0:T(8,128)(2,1)S(1)} %collective-permute-done.2.refs_0_), channel_id=1, source_target_pairs={{0,1},{1,0},{2,3},{3,2},{4,5},{5,4},{6,7},{7,6},{8,9},{9,8},{10,11... | collective-permute-start | bytes 835592 | tf_op jit(solution)/shard_map/ppermute | solution.py:207
  25.7 18.8 %collective-permute-start.5 = (bf16[272,512]{1,0:T(8,128)(2,1)S(1)}, bf16[272,512]{1,0:T(8,128)(2,1)S(1)}, u32[]{:S(2)}, u32[]{:S(2)}) collective-permute-start(bf16[272,512]{1,0:T(8,128)(2,1)S(1)} %collective-permute-done.4.refs_0_), channel_id=1, source_target_pairs={{0,1},{1,0},{2,3},{3,2},{4,5},{5,4},{6,7},{7,6},{8,9},{9,8},{10,11... | collective-permute-start | bytes 835592 | tf_op jit(solution)/shard_map/ppermute | solution.py:207
  32.9 11.6 %copy-start.7 = (f32[16,128]{1,0:T(8,128)}, f32[16,128]{1,0:T(8,128)S(1)}, u32[]{:S(2)}) copy-start(f32[16,128]{1,0:T(8,128)S(1)} %quadratic.5.refs_0_) | copy-start | bytes 24580
  36.6 7.9 %copy-start.3 = (f32[4,128]{1,0:T(4,128)}, f32[4,128]{1,0:T(4,128)S(1)}, u32[]{:S(2)}) copy-start(f32[4,128]{1,0:T(4,128)S(1)} %quadratic.6.refs_1_) | copy-start | bytes 6148
  40.2 4.3 %copy-start.4 = (f32[4,128]{1,0:T(4,128)}, f32[4,128]{1,0:T(4,128)S(1)}, u32[]{:S(2)}) copy-start(f32[4,128]{1,0:T(4,128)S(1)} %quadratic.8.refs_3_) | copy-start | bytes 6148
  43.9 0.6 copy-start.5
  48.2 0.6 copy-start.6
  50.1 4.3 %collective-permute-start.6 = (f32[1,128]{1,0:T(1,128)}, f32[1,128]{1,0:T(1,128)S(1)}, u32[]{:S(2)}, u32[]{:S(2)}) collective-permute-start(f32[1,128]{1,0:T(1,128)} %get-tuple-element.5), channel_id=1, source_target_pairs={{0,4},{4,0},{8,12},{12,8},{16,20},{20,16},{24,28},{28,24},{1,5},{5... | collective-permute-start | bytes 1544 | tf_op jit(solution)/shard_map/ppermute | solution.py:207
  55.1 3.6 %collective-permute-start.7 = (f32[1,128]{1,0:T(1,128)S(1)}, f32[1,128]{1,0:T(1,128)S(1)}, u32[]{:S(2)}, u32[]{:S(2)}) collective-permute-start(f32[1,128]{1,0:T(1,128)S(1)} %add.6), channel_id=1, source_target_pairs={{0,8},{4,12},{8,0},{12,4},{16,24},{20,28},{24,16},{28,20},{1,9},{5... | collective-permute-start | bytes 1544 | tf_op jit(solution)/shard_map/ppermute | solution.py:207
  58.6 4.5 %copy-start.9 = (f32[1,128]{1,0:T(1,128)}, f32[1,128]{1,0:T(1,128)S(1)}, u32[]{:S(2)}) copy-start(f32[1,128]{1,0:T(1,128)S(1)} %add.7.mine) | copy-start | bytes 1540
  58.6 4.5 %collective-permute-start.8 = (f32[1,128]{1,0:T(1,128)S(1)}, f32[1,128]{1,0:T(1,128)S(1)}, u32[]{:S(2)}, u32[]{:S(2)}) collective-permute-start(f32[1,128]{1,0:T(1,128)S(1)} %add.7.mine), channel_id=1, source_target_pairs={{0,16},{4,20},{8,24},{12,28},{16,0},{20,4},{24,8},{28,12},{1,17},{... | collective-permute-start | bytes 1544 | tf_op jit(solution)/shard_map/ppermute | solution.py:207
  63.1 0.6 copy-start.10
